TPU v7x, 128 devices: a whole 4x4x4 slice. The times are simulated.
128 devices in a mesh: rep: 16 (over x, y_lo, core), tp: 8 (over z, y_hi).
Axes of the slice: x: 4, y: 4 (y_hi: 2, y_lo: 2; y = y_hi * 2 + y_lo), z: 4, core: 2. Of those that a mesh axis runs over, the one named last changes fastest.
Arguments:
- context: bfloat16 [32768, 5120], P('rep', 'tp'), may hold values from -6 to 6
- out_grad: bfloat16 [32768, 5120], P('rep', 'tp'), may hold values from -6 to 6
- rewards: int32 [8, 64], P(None, 'rep'), may hold values from 0 to 1
- master: float32 [5120, 5120], P('rep', 'tp'), may hold values from -0.078125 to 0.078125
- first_moment: float32 [5120, 5120], P('rep', 'tp'), may hold values from -0.03125 to 0.03125
- second_moment: float32 [5120, 5120], P('rep', 'tp'), may hold values from 3.0517577e-07 to 3.0517578e-05
- inputs: bfloat16 [4, 512, 5120], P(None, 'rep'), may hold values from -6 to 6
- w_query: bfloat16 [5120, 5120], P(None, 'tp'), may hold values from -0.078125 to 0.078125
- w_key: bfloat16 [5120, 1024], P(None, 'tp'), may hold values from -0.078125 to 0.078125
- w_value: bfloat16 [5120, 1024], P(None, 'tp'), may hold values from -0.078125 to 0.078125
- cache_keys: bfloat16 [512, 256, 1024], P('rep', None, 'tp'), may hold values from -400 to 400
- cache_values: bfloat16 [512, 256, 1024], P('rep', None, 'tp'), may hold values from -24 to 24
- lengths: int32 [64], P('rep'), may hold values from 64 to 256
Outputs:
- decoded: bfloat16 [4, 512, 5120], P(None, 'rep')
- adam_step: float32 [5120, 5120], P('rep', 'tp')
All inputs are finite; a program needn't handle non-finite values.
Results may differ from a plain program's by a relative error of at most 0.0088.
Values may be sent and summed in bfloat16 or wider, within the bound.
A program may use at most 128 MiB of HBM per device.

v0:
```python
import jax
import jax.numpy as jnp
from jax import lax
from jax.sharding import PartitionSpec as P

HEAD_DIM = 128
rope_base = 1000000.0
first_beta = 0.9
second_beta = 0.95
adam_epsilon = 1e-08
step_count = 10
learn_rate = 0.001


def from_everyone(array, axis):
    devices = lax.axis_size(axis)
    return lax.all_to_all(
        jnp.broadcast_to(array[None], (devices, *array.shape)), axis, 0, 0, tiled=True
    )


def of_everyone(array, axis):
    everything = from_everyone(array, axis)
    return jnp.sum(everything, axis=0)


def laid_out(tiles, dim):
    tiles = jnp.moveaxis(tiles, 0, dim)
    lengths = tiles.shape
    return tiles.reshape(*lengths[:dim], lengths[dim] * lengths[dim + 1], *lengths[dim + 2 :])


def collect(array, axis, dim):
    return laid_out(from_everyone(array, axis), dim)


def split_up(array, dim, devices):
    before, after = (array.shape[:dim], array.shape[dim + 1 :])
    return jnp.moveaxis(array.reshape(*before, devices, -1, *after), dim, 0)


def sum_at_owner(array, axis, dim):
    tiles = split_up(array, dim, lax.axis_size(axis))
    arrived = lax.all_to_all(tiles, axis, split_axis=0, concat_axis=0, tiled=True)
    return arrived.sum(axis=0)


def rotate(vectors, positions):
    half_dim = vectors.shape[-1] // 2
    frequency = rope_base ** (-2.0 * jnp.arange(half_dim, dtype=jnp.float32) / vectors.shape[-1])
    angles = positions[..., None].astype(jnp.float32) * frequency
    cosine_table = jnp.cos(angles)
    sine_table = jnp.sin(angles)
    former = vectors[..., :half_dim]
    latter = vectors[..., half_dim:]
    return jnp.concatenate(
        [former * cosine_table - latter * sine_table, latter * cosine_table + former * sine_table],
        axis=-1,
    )


def attend(queries, old_keys, old_values, new_keys, new_values, live_mask):
    score_scale = HEAD_DIM ** (-0.5)
    step_total = queries.shape[0]
    cache_scores = (
        jnp.einsum("tsgqd,scgd->tsgqc", queries, old_keys, preferred_element_type=jnp.float32)
        * score_scale
    )
    cache_scores = jnp.where(live_mask[None, :, None, None, :], cache_scores, -1e30)
    recent = (
        jnp.einsum("tsgqd,usgd->tsgqu", queries, new_keys, preferred_element_type=jnp.float32)
        * score_scale
    )
    causal = jnp.arange(step_total)[:, None] >= jnp.arange(step_total)[None, :]
    recent = jnp.where(causal[:, None, None, None, :], recent, -1e30)
    row_peak = jnp.maximum(jnp.max(cache_scores, axis=-1), jnp.max(recent, axis=-1))[..., None]
    cache_exp = jnp.exp(cache_scores - row_peak)
    recent_exp = jnp.exp(recent - row_peak)
    denominator = jnp.sum(cache_exp, axis=-1, keepdims=True) + jnp.sum(
        recent_exp, axis=-1, keepdims=True
    )
    cache_weight = (cache_exp / denominator).astype(jnp.bfloat16)
    recent_weight = (recent_exp / denominator).astype(jnp.bfloat16)
    attended = jnp.einsum(
        "tsgqc,scgd->tsgqd", cache_weight, old_values, preferred_element_type=jnp.float32
    )
    attended = attended + jnp.einsum(
        "tsgqu,usgd->tsgqd", recent_weight, new_values, preferred_element_type=jnp.float32
    )
    return attended.astype(jnp.bfloat16)


def per_device(
    context,
    out_grad,
    rewards,
    master,
    first_moment,
    second_moment,
    inputs,
    w_query,
    w_key,
    w_value,
    cache_keys,
    cache_values,
    lengths,
):
    replicas = lax.axis_size("rep")
    prompt_count, local_group = rewards.shape
    totals = of_everyone(jnp.sum(rewards, axis=1), "rep")
    group_size = local_group * replicas
    advantage = rewards.astype(jnp.float32) - totals.astype(jnp.float32)[:, None] / group_size
    token_local = context.shape[0]
    per_token = jnp.repeat(advantage.reshape(-1), token_local // (prompt_count * local_group)) / (
        token_local * replicas
    )
    scaled = (out_grad.astype(jnp.float32) * per_token[:, None]).astype(jnp.bfloat16)
    features = lax.all_gather(context, "tp", axis=1, tiled=True)
    gradient = lax.psum_scatter(
        lax.dot_general(
            features, scaled, (((0,), (0,)), ((), ())), preferred_element_type=jnp.float32
        ).astype(jnp.bfloat16),
        "rep",
        scatter_dimension=0,
        tiled=True,
    ).astype(jnp.float32)
    moment_new = first_beta * first_moment + (1.0 - first_beta) * gradient
    square_new = second_beta * second_moment + (1.0 - second_beta) * gradient * gradient
    adam_step = (
        moment_new
        / (1.0 - first_beta**step_count)
        / (jnp.sqrt(square_new / (1.0 - second_beta**step_count)) + adam_epsilon)
    )
    weight = (master - learn_rate * adam_step).astype(jnp.bfloat16)
    step_total, seq_local, model_width = inputs.shape
    local_heads = w_query.shape[1] // HEAD_DIM
    local_kv = w_key.shape[1] // HEAD_DIM
    flat_rows = inputs.reshape(step_total * seq_local, model_width)
    queries = jnp.dot(flat_rows, w_query, preferred_element_type=jnp.float32).reshape(
        step_total, seq_local, local_heads, HEAD_DIM
    )
    key_new = jnp.dot(flat_rows, w_key, preferred_element_type=jnp.float32).reshape(
        step_total, seq_local, local_kv, HEAD_DIM
    )
    value_new = (
        jnp.dot(flat_rows, w_value, preferred_element_type=jnp.float32)
        .reshape(step_total, seq_local, local_kv, HEAD_DIM)
        .astype(jnp.bfloat16)
    )
    seq_length = jnp.repeat(lengths, seq_local // lengths.shape[0])
    positions = seq_length[None, :] + jnp.arange(step_total, dtype=jnp.int32)[:, None]
    queries = rotate(queries, positions[:, :, None]).astype(jnp.bfloat16)
    queries = queries.reshape(step_total, seq_local, local_kv, local_heads // local_kv, HEAD_DIM)
    key_new = rotate(key_new, positions[:, :, None]).astype(jnp.bfloat16)
    slot_total = cache_keys.shape[1]
    old_keys = cache_keys.reshape(seq_local, slot_total, local_kv, HEAD_DIM)
    old_values = cache_values.reshape(seq_local, slot_total, local_kv, HEAD_DIM)
    live_mask = jnp.arange(slot_total, dtype=jnp.int32)[None, :] < seq_length[:, None]
    attended = attend(queries, old_keys, old_values, key_new, value_new, live_mask)
    attended = attended.reshape(step_total * seq_local, local_heads * HEAD_DIM)
    all_heads = collect(attended, "tp", 1)
    feature_rows = lax.all_to_all(all_heads, "rep", split_axis=1, concat_axis=0, tiled=True)
    own_columns = sum_at_owner(
        jnp.dot(feature_rows, weight, preferred_element_type=jnp.float32), "rep", 0
    )
    decoded = collect(own_columns.astype(jnp.bfloat16), "tp", 1)
    return (decoded.reshape(step_total, seq_local, model_width), adam_step)


def solution(mesh):
    placed = (
        P("rep", "tp"),
        P("rep", "tp"),
        P(None, "rep"),
        P("rep", "tp"),
        P("rep", "tp"),
        P("rep", "tp"),
        P(None, "rep", None),
        P(None, "tp"),
        P(None, "tp"),
        P(None, "tp"),
        P("rep", None, "tp"),
        P("rep", None, "tp"),
        P("rep"),
    )
    return jax.shard_map(
        per_device,
        mesh=mesh,
        in_specs=placed,
        out_specs=(P(None, "rep", None), P("rep", "tp")),
        check_vma=False,
    )
```

profile of v0, /device:TPU:0, one launch (start us, length us, event | category | flops | bytes accessed | tf_op | source)
XLA Modules:
  0.0 483.4 jit_solution(15974922212269263185)
XLA Ops:
  7.2 0.0 copy-start
  7.2 0.0 copy-start.5
  7.2 0.0 all-gather.2.cloned.1.call-start
  7.2 0.7 all-gather.2.cloned.1.call-update
  7.9 0.0 reduce-scatter.4.cloned.1.call-start
  8.0 0.0 copy-done.5
  8.0 11.4 %all_to_all.37 = s32[16,1,8]{2,1,0:T(1,128)S(1)} all-to-all(s32[16,1,8]{2,1,0:T(1,128)S(1)} %broadcast_in_dim.69), channel_id=1, replica_groups=mesh['rep'=16,'tp'=8] {'rep'}, dimensions={0} | all-to-all | bytes 1024 | tf_op jit(solution)/shard_map/all_to_all | solution.py:17
  19.5 0.1 copy.87
  19.6 0.1 div.61
  19.7 0.1 broadcast_in_dim.70
  19.7 0.1 div.62
  19.8 212.7 %all-gather.2.cloned.1.call-done = bf16[2048,5120]{1,0:T(8,128)(2,1)} async-done(((bf16[2048,640]{1,0:T(8,128)(2,1)}), bf16[2048,5120]{1,0:T(8,128)(2,1)}) %all-gather.2.cloned.1.call-update) | async-done | bytes 20971536 | tf_op jit(solution)/shard_map/all_gather | solution.py:118
  232.5 20.7 %fusion = bf16[5120,640]{0,1:T(8,128)(2,1)} fusion(bf16[2048,5120]{1,0:T(8,128)(2,1)} %all-gather.2.cloned.1.call-done, bf16[2048,640]{1,0:T(8,128)(2,1)} %param.14, f32[2048]{0:T(1024)S(1)} %div.62), kind=kOutput, calls=%fused_computation.1 | convolution fusion | flops 13428981760 | bytes 30154752 | tf_op jit(solution)/shard_map/dot_general | solution.py:120
  253.2 9.5 %copy.104 = bf16[5120,640]{1,0:T(8,128)(2,1)} copy(bf16[5120,640]{0,1:T(8,128)(2,1)} %fusion) | data formatting | bytes 13107200
  262.7 0.0 copy-start.6
  262.7 0.0 reduce-scatter.4.cloned.1.call-update
  262.7 0.6 copy-done.6
  263.4 0.1 broadcast_in_dim.36
  263.4 0.1 lt.20
  263.5 0.0 copy-start.1
  263.5 9.7 %copy.78 = bf16[5120,640]{0,1:T(8,128)(2,1)} copy(bf16[5120,640]{1,0:T(8,128)(2,1)} %param.20) | data formatting | bytes 13107200 | tf_op args[7]
  273.3 0.0 copy-done.1
  273.3 1.8 fusion.32
  275.1 0.3 fusion.71
  275.4 0.1 maximum_bitcast_fusion
  275.5 0.3 multiply_cosine_fusion.1
  275.8 5.1 %fusion.12 = f32[4,32,5,128]{3,1,2,0:T(8,128)S(1)} fusion(bf16[5,128,5120,1]{2,1,0,3:T(8,128)(2,1)} %bitcast.105, bf16[4,32,5120]{2,1,0:T(8,128)(2,1)S(1)} %copy-done.1), kind=kOutput, calls=%fused_computation.11 | convolution fusion | flops 838860800 | bytes 8192000 | tf_op jit(solution)/shard_map/dot_general | solution.py:139
  280.9 0.2 subtract_convert_fusion.1
  281.1 0.1 pad_maximum_fusion
  281.2 0.1 iota_compare_fusion
  281.3 1.3 fusion.74
  282.6 0.0 copy-done
  282.6 0.0 copy-start.2
  282.7 0.8 fusion.73
  283.5 0.3 fusion.57
  283.8 0.5 fusion.49
  284.2 0.0 copy-done.2
  284.3 0.5 fusion.38
  284.8 0.7 copy-done.7
  285.4 0.6 fusion.26
  286.1 0.4 fusion.30
  286.5 0.2 copy.84
  286.7 0.2 broadcast_in_dim.68
  286.9 0.0 copy-start.3
  286.9 38.0 %all_to_all.38 = bf16[8,128,640]{1,2,0:T(8,128)(2,1)} all-to-all(bf16[8,128,640]{1,2,0:T(8,128)(2,1)S(1)} %broadcast_in_dim.68), channel_id=1, replica_groups=mesh['rep'=16,'tp'=8] {'tp'}, dimensions={0} | all-to-all | bytes 2621440 | tf_op jit(solution)/shard_map/all_to_all | solution.py:17
  324.9 6.1 %all-to-all-start.1 = ((bf16[128,16,320]{0,2,1:T(8,128)(2,1)}), bf16[128,16,320]{0,2,1:T(8,128)(2,1)}, u32[]{:S(2)}, u32[]{:S(2)}) async-start(bf16[128,16,320]{0,2,1:T(8,128)(2,1)} %bitcast.27), calls=%async_computation.1 | async-start | bytes 2621440 | tf_op jit(solution)/shard_map/all_to_all | solution.py:162
  331.0 0.0 copy-done.3
  331.0 1.3 copy.89
  332.3 2.5 copy.85
  334.9 0.0 copy-done.4
  334.9 1.3 copy.88
  336.1 33.8 %reduce-scatter.4.cloned.1.call-done = bf16[320,640]{1,0:T(8,128)(2,1)} async-done(((bf16[5120,640]{1,0:T(8,128)(2,1)}), bf16[320,640]{1,0:T(8,128)(2,1)}) %reduce-scatter.4.cloned.1.call-update) | async-done | bytes 409616
  370.0 2.0 copy.105
  371.9 2.3 fusion.44
  374.2 0.0 all-to-all-done.1
  374.2 3.4 fusion.14
  377.6 67.4 %all_to_all.39 = f32[16,128,640]{2,1,0:T(8,128)} all-to-all(f32[16,128,640]{2,1,0:T(8,128)S(1)} %fusion.14), channel_id=1, replica_groups=mesh['rep'=16,'tp'=8] {'rep'}, dimensions={0} | all-to-all | bytes 10485760 | tf_op jit(solution)/shard_map/all_to_all | solution.py:44
  445.0 2.7 reduce_sum.49
  447.8 1.2 broadcast_in_dim.71
  448.9 4.3 all-to-all-start.4
  453.2 1.2 copy.92
  454.4 18.6 %all-to-all-done.4 = bf16[8,128,640]{2,1,0:T(8,128)(2,1)} async-done(((bf16[8,128,640]{2,1,0:T(8,128)(2,1)}), bf16[8,128,640]{2,1,0:T(8,128)(2,1)}, u32[]{:S(2)}, u32[]{:S(2)}) %all-to-all-start.4) | async-done | bytes 1310752 | tf_op jit(solution)/shard_map/all_to_all | solution.py:17
  473.0 2.1 copy.91
  475.1 1.5 reshape_reshape.3
  (14 shorter events, 0.2 us)
Async XLA Ops:
  7.2 275.5 %copy-start = (bf16[32,256,128]{2,1,0:T(8,128)(2,1)S(1)}, bf16[32,256,128]{2,1,0:T(8,128)(2,1)}, u32[]{:S(2)}) copy-start(bf16[32,256,128]{2,1,0:T(8,128)(2,1)} %param.23) | copy-start | bytes 6291460
  7.2 0.8 copy-start.5
  7.2 225.3 %all-gather.2.cloned.1.call-start = ((), (), s32[]{:S(2)}) async-start(), calls=%async_computation.6 | async-start | bytes 23592960 | tf_op jit(solution)/shard_map/all_gather | solution.py:118
  7.9 362.0 %reduce-scatter.4.cloned.1.call-start = ((), (), s32[]{:S(2)}) async-start(), calls=%async_computation.7 | async-start | bytes 6963200
  262.7 0.7 copy-start.6
  263.5 9.8 %copy-start.1 = (bf16[4,32,5120]{2,1,0:T(8,128)(2,1)S(1)}, bf16[4,32,5120]{2,1,0:T(8,128)(2,1)}, u32[]{:S(2)}) copy-start(bf16[4,32,5120]{2,1,0:T(8,128)(2,1)} %param.19) | copy-start | bytes 3932164
  282.6 1.6 copy-start.2
  283.8 1.7 copy-start.7
  286.9 44.2 %copy-start.3 = (f32[320,640]{1,0:T(8,128)S(1)}, f32[320,640]{1,0:T(8,128)}, u32[]{:S(2)}) copy-start(f32[320,640]{1,0:T(8,128)} %param.16) | copy-start | bytes 2457604
  324.9 49.3 %all-to-all-start.1 = ((bf16[128,16,320]{0,2,1:T(8,128)(2,1)}), bf16[128,16,320]{0,2,1:T(8,128)(2,1)}, u32[]{:S(2)}, u32[]{:S(2)}) async-start(bf16[128,16,320]{0,2,1:T(8,128)(2,1)} %bitcast.27), calls=%async_computation.1 | async-start | bytes 2621440 | tf_op jit(solution)/shard_map/all_to_all | solution.py:162
  332.3 2.5 copy-start.4
  448.9 24.1 %all-to-all-start.4 = ((bf16[8,128,640]{2,1,0:T(8,128)(2,1)}), bf16[8,128,640]{2,1,0:T(8,128)(2,1)}, u32[]{:S(2)}, u32[]{:S(2)}) async-start(bf16[8,128,640]{2,1,0:T(8,128)(2,1)} %broadcast_in_dim.71), calls=%async_computation.4 | async-start | bytes 2621440 | tf_op jit(solution)/shard_map/all_to_all | solution.py:17
Sparse Core Ops, SparseCore 0:
  10.4 222.0 all-gather.1
  262.9 107.0 reduce-scatter.3
where the time goes:
time: 484 us; the launch traced here: 483 us
  waiting for transfers between devices  266 us (55%)
  blocking collectives  117 us (24%)
  matrix products  34.6 us (7%)
  local copies, waits for them, and re-layouts  34.5 us (7%)
  between operations  14.3 us (3%)
  starting transfers between devices  10.4 us (2%)
  other arithmetic  6.95 us (1%)
    all_gather x1, waiting for transfers between devices, per_device(): features = lax.all_gather(context, 'tp', axis=1, tiled=True)  213 us
    all_to_all x1, blocking collectives, sum_at_owner(): lax.all_to_all(tiles, axis, split_axis=0, concat_axis=0, tiled=True)  67.4 us
    all_to_all x2, blocking collectives, from_everyone(): lax.all_to_all(jnp.broadcast_to(array[None], (devices, *array.shape)), ax...  49.5 us
    unnamed x3, waiting for transfers between devices  34.5 us
    unnamed x24, local copies, waits for them, and re-layouts  28.9 us
    dot_general x1, matrix products, per_device(): lax.dot_general(features, scaled, (((0,), (0,)), ((), ())), preferred_ele...  20.7 us
    all_to_all x1, waiting for transfers between devices, from_everyone(): lax.all_to_all(jnp.broadcast_to(array[None], (devices, *array.shape)), ax...  18.6 us
  transfers between devices with their start and end apart: 4, of which 3 were waited for; matrix products, arithmetic and copies ran while one was open for 7% of the time, Pallas kernels for 0%

commit v1 on v0

--- a/solution.py
+++ b/solution.py
@@ -115,7 +115,8 @@
         token_local * replicas
     )
     scaled = (out_grad.astype(jnp.float32) * per_token[:, None]).astype(jnp.bfloat16)
-    features = lax.all_gather(context, "tp", axis=1, tiled=True)
+    sent = jnp.stack([context] * lax.axis_size("tp"))
+    features = jnp.concatenate(lax.all_to_all(sent, "tp", 0, 0), axis=1)
     gradient = lax.psum_scatter(
         lax.dot_general(
             features, scaled, (((0,), (0,)), ((), ())), preferred_element_type=jnp.float32

time: 484 us -> 519 us (1.072)
  waiting for transfers between devices: 266 us -> 283 us
  starting transfers between devices: 10.4 us -> 25.2 us
  local copies, waits for them, and re-layouts: 34.5 us -> 47.8 us
  blocking collectives: 117 us -> 105 us
    all_to_all x0 -> x1, waiting for transfers between devices: none -> 230 us  [per_device(): features = jnp.concatenate(lax.all_to_all(sent, 'tp', 0, 0), axis=1)]
    all_gather x1 -> x0, waiting for transfers between devices: 213 us -> none  [per_device(): features = lax.all_gather(context, 'tp', axis=1, tiled=True)]
    all_to_all x2 -> x1, blocking collectives: 49.5 us -> 37.9 us  [from_everyone(): lax.all_to_all(jnp.broadcast_to(array[None], (devices, *array.shape)), ax...]
    another operation x0 -> x1, local copies, waits for them, and re-layouts: none -> 8.39 us  [per_device(): sent = jnp.stack([context] * lax.axis_size('tp'))]
    all_to_all x0 -> x1, starting transfers between devices: none -> 7.78 us  [per_device(): features = jnp.concatenate(lax.all_to_all(sent, 'tp', 0, 0), axis=1)]
    all_to_all x1 -> x2, starting transfers between devices: 4.26 us -> 11.5 us  [from_everyone(): lax.all_to_all(jnp.broadcast_to(array[None], (devices, *array.shape)), ax...]
    unnamed x24 -> x25, local copies, waits for them, and re-layouts: 28.9 us -> 33.3 us
    unnamed x3 -> x2, waiting for transfers between devices: 34.5 us -> 32.5 us
  transfers between devices with their start and end apart: 4 -> 5, of which waited for: 3 -> 4; matrix products, arithmetic and copies ran while one was open for 7% -> 7% of each run, Pallas kernels for 0% -> 0%
where the time goes in v1:
time: 519 us; the launch traced here: 518 us
  waiting for transfers between devices  283 us (55%)
  blocking collectives  105 us (20%)
  local copies, waits for them, and re-layouts  47.8 us (9%)
  matrix products  35.1 us (7%)
  starting transfers between devices  25.2 us (5%)
  between operations  14.3 us (3%)
  other arithmetic  7.78 us (1%)
    all_to_all x1, waiting for transfers between devices, per_device(): features = jnp.concatenate(lax.all_to_all(sent, 'tp', 0, 0), axis=1)  230 us
    all_to_all x1, blocking collectives, sum_at_owner(): lax.all_to_all(tiles, axis, split_axis=0, concat_axis=0, tiled=True)  67.3 us
    all_to_all x1, blocking collectives, from_everyone(): lax.all_to_all(jnp.broadcast_to(array[None], (devices, *array.shape)), ax...  37.9 us
    unnamed x25, local copies, waits for them, and re-layouts  33.3 us
    unnamed x2, waiting for transfers between devices  32.5 us
    dot_general x1, matrix products, per_device(): lax.dot_general(features, scaled, (((0,), (0,)), ((), ())), preferred_ele...  21.2 us
    all_to_all x2, waiting for transfers between devices, from_everyone(): lax.all_to_all(jnp.broadcast_to(array[None], (devices, *array.shape)), ax...  19.9 us
    all_to_all x2, starting transfers between devices, from_everyone(): lax.all_to_all(jnp.broadcast_to(array[None], (devices, *array.shape)), ax...  11.5 us
  transfers between devices with their start and end apart: 5, of which 4 were waited for; matrix products, arithmetic and copies ran while one was open for 7% of the time, Pallas kernels for 0%

profile of v1, /device:TPU:0, one launch (start us, length us, event | category | flops | bytes accessed | tf_op | source)
XLA Modules:
  0.0 518.0 jit_solution(10915479923971549798)
XLA Ops:
  7.2 0.0 copy-start
  7.2 0.8 reduce_sum.47
  8.0 0.6 broadcast_in_dim.69
  8.6 5.5 %all-to-all-start.2 = ((s32[16,1,8]{2,1,0:T(1,128)}), s32[16,1,8]{2,1,0:T(1,128)S(1)}, u32[]{:S(2)}, u32[]{:S(2)}) async-start(s32[16,1,8]{2,1,0:T(1,128)} %broadcast_in_dim.69), calls=%async_computation.2 | async-start | bytes 16384 | tf_op jit(solution)/shard_map/all_to_all | solution.py:17
  14.2 4.5 copy.92
  18.7 1.5 all-to-all-done.2
  20.2 8.4 %stack.2 = bf16[8,2048,640]{1,2,0:T(8,128)(2,1)} broadcast(bf16[2048,640]{0,1:T(8,128)(2,1)} %copy.92), dimensions={1,2} | broadcast | bytes 23592960 | tf_op jit(solution)/shard_map/stack | solution.py:118
  28.6 7.8 %all-to-all-start.3 = ((bf16[8,2048,640]{1,2,0:T(8,128)(2,1)}), bf16[8,2048,640]{1,2,0:T(8,128)(2,1)}, u32[]{:S(2)}, u32[]{:S(2)}) async-start(bf16[8,2048,640]{1,2,0:T(8,128)(2,1)} %stack.2), calls=%async_computation.3 | async-start | bytes 41943040 | tf_op jit(solution)/shard_map/all_to_all | solution.py:119
  36.4 0.0 reduce-scatter.4.cloned.1.call-start
  36.4 0.0 copy-done.5
  36.5 0.1 copy.91
  36.5 0.1 div.61
  36.6 0.1 broadcast_in_dim.70
  36.7 0.1 div.62
  36.8 230.4 %all-to-all-done.3 = bf16[8,2048,640]{1,2,0:T(8,128)(2,1)} async-done(((bf16[8,2048,640]{1,2,0:T(8,128)(2,1)}), bf16[8,2048,640]{1,2,0:T(8,128)(2,1)}, u32[]{:S(2)}, u32[]{:S(2)}) %all-to-all-start.3) | async-done | bytes 20971552 | tf_op jit(solution)/shard_map/all_to_all | solution.py:119
  267.2 21.2 %fusion = bf16[5120,640]{0,1:T(8,128)(2,1)} fusion(bf16[2048,5120]{0,1:T(8,128)(2,1)} %bitcast.30, bf16[2048,640]{1,0:T(8,128)(2,1)} %param.14, f32[2048]{0:T(1024)S(1)} %div.62), kind=kOutput, calls=%fused_computation.1 | convolution fusion | flops 13428981760 | bytes 30154752 | tf_op jit(solution)/shard_map/dot_general | solution.py:121
  288.4 9.5 %copy.109 = bf16[5120,640]{1,0:T(8,128)(2,1)} copy(bf16[5120,640]{0,1:T(8,128)(2,1)} %fusion) | data formatting | bytes 13107200
  297.9 0.0 reduce-scatter.4.cloned.1.call-update
  297.9 0.6 copy-done.6
  298.5 0.1 broadcast_in_dim.36
  298.6 0.1 lt.20
  298.7 9.7 %copy.82 = bf16[5120,640]{0,1:T(8,128)(2,1)} copy(bf16[5120,640]{1,0:T(8,128)(2,1)} %param.20) | data formatting | bytes 13107200 | tf_op args[7]
  308.4 0.0 copy-done.1
  308.4 1.8 fusion.32
  310.3 0.3 fusion.71
  310.6 0.1 maximum_bitcast_fusion
  310.7 0.3 multiply_cosine_fusion.1
  311.0 5.1 fusion.12
  316.1 0.2 subtract_convert_fusion.1
  316.3 0.1 pad_maximum_fusion
  316.4 0.1 iota_compare_fusion
  316.5 1.3 fusion.74
  317.8 0.0 copy-done
  317.8 0.0 copy-start.2
  317.8 0.8 fusion.73
  318.6 0.3 fusion.57
  318.9 0.5 fusion.49
  319.4 0.0 copy-done.2
  319.4 0.5 fusion.38
  319.9 0.6 copy-done.7
  320.5 0.6 fusion.26
  321.2 0.4 fusion.30
  321.6 0.2 copy.88
  321.8 0.2 broadcast_in_dim.68
  321.9 0.0 copy-start.3
  322.0 37.9 %all_to_all.42 = bf16[8,128,640]{1,2,0:T(8,128)(2,1)} all-to-all(bf16[8,128,640]{1,2,0:T(8,128)(2,1)S(1)} %broadcast_in_dim.68), channel_id=1, replica_groups=mesh['rep'=16,'tp'=8] {'tp'}, dimensions={0} | all-to-all | bytes 2621440 | tf_op jit(solution)/shard_map/all_to_all | solution.py:17
  359.8 5.9 %all-to-all-start.1 = ((bf16[128,16,320]{0,2,1:T(8,128)(2,1)}), bf16[128,16,320]{0,2,1:T(8,128)(2,1)}, u32[]{:S(2)}, u32[]{:S(2)}) async-start(bf16[128,16,320]{0,2,1:T(8,128)(2,1)} %bitcast.27), calls=%async_computation.1 | async-start | bytes 2621440 | tf_op jit(solution)/shard_map/all_to_all | solution.py:163
  365.7 0.0 copy-done.3
  365.7 1.3 copy.89
  367.0 2.5 copy.93
  369.5 1.3 copy.94
  370.8 32.4 %reduce-scatter.4.cloned.1.call-done = bf16[320,640]{1,0:T(8,128)(2,1)} async-done(((bf16[5120,640]{1,0:T(8,128)(2,1)}), bf16[320,640]{1,0:T(8,128)(2,1)}) %reduce-scatter.4.cloned.1.call-update) | async-done | bytes 409616
  403.3 2.0 copy.110
  405.2 2.3 fusion.44
  407.5 0.0 all-to-all-done.1
  407.5 3.4 fusion.14
  410.9 67.3 %all_to_all.43 = f32[16,128,640]{2,1,0:T(8,128)} all-to-all(f32[16,128,640]{2,1,0:T(8,128)S(1)} %fusion.14), channel_id=1, replica_groups=mesh['rep'=16,'tp'=8] {'rep'}, dimensions={0} | all-to-all | bytes 10485760 | tf_op jit(solution)/shard_map/all_to_all | solution.py:44
  478.2 2.7 reduce_sum.49
  480.9 1.2 broadcast_in_dim.71
  482.1 6.0 %all-to-all-start.5 = ((bf16[8,128,640]{2,1,0:T(8,128)(2,1)}), bf16[8,128,640]{2,1,0:T(8,128)(2,1)}, u32[]{:S(2)}, u32[]{:S(2)}) async-start(bf16[8,128,640]{2,1,0:T(8,128)(2,1)} %broadcast_in_dim.71), calls=%async_computation.5 | async-start | bytes 2621440 | tf_op jit(solution)/shard_map/all_to_all | solution.py:17
  488.1 1.2 copy.97
  489.3 18.4 %all-to-all-done.5 = bf16[8,128,640]{2,1,0:T(8,128)(2,1)} async-done(((bf16[8,128,640]{2,1,0:T(8,128)(2,1)}), bf16[8,128,640]{2,1,0:T(8,128)(2,1)}, u32[]{:S(2)}, u32[]{:S(2)}) %all-to-all-start.5) | async-done | bytes 1310752 | tf_op jit(solution)/shard_map/all_to_all | solution.py:17
  507.6 2.1 copy.96
  509.7 1.5 reshape_reshape.3
  (16 shorter events, 0.2 us)
Async XLA Ops:
  7.2 310.6 %copy-start = (bf16[32,256,128]{2,1,0:T(8,128)(2,1)S(1)}, bf16[32,256,128]{2,1,0:T(8,128)(2,1)}, u32[]{:S(2)}) copy-start(bf16[32,256,128]{2,1,0:T(8,128)(2,1)} %param.23) | copy-start | bytes 6291460
  8.6 11.5 %all-to-all-start.2 = ((s32[16,1,8]{2,1,0:T(1,128)}), s32[16,1,8]{2,1,0:T(1,128)S(1)}, u32[]{:S(2)}, u32[]{:S(2)}) async-start(s32[16,1,8]{2,1,0:T(1,128)} %broadcast_in_dim.69), calls=%async_computation.2 | async-start | bytes 16384 | tf_op jit(solution)/shard_map/all_to_all | solution.py:17
  28.6 7.9 %copy-start.5 = (s32[8,4]{0,1:T(4,128)S(1)}, s32[8,4]{0,1:T(4,128)}, u32[]{:S(2)}) copy-start(s32[8,4]{0,1:T(4,128)} %param.15) | copy-start | bytes 388
  28.6 238.6 %all-to-all-start.3 = ((bf16[8,2048,640]{1,2,0:T(8,128)(2,1)}), bf16[8,2048,640]{1,2,0:T(8,128)(2,1)}, u32[]{:S(2)}, u32[]{:S(2)}) async-start(bf16[8,2048,640]{1,2,0:T(8,128)(2,1)} %stack.2), calls=%async_computation.3 | async-start | bytes 41943040 | tf_op jit(solution)/shard_map/all_to_all | solution.py:119
  36.4 366.9 %reduce-scatter.4.cloned.1.call-start = ((), (), s32[]{:S(2)}) async-start(), calls=%async_computation.7 | async-start | bytes 6963200
  297.9 0.7 copy-start.6
  298.7 9.7 %copy-start.1 = (bf16[4,32,5120]{2,1,0:T(8,128)(2,1)S(1)}, bf16[4,32,5120]{2,1,0:T(8,128)(2,1)}, u32[]{:S(2)}) copy-start(bf16[4,32,5120]{2,1,0:T(8,128)(2,1)} %param.19) | copy-start | bytes 3932164
  317.8 1.6 copy-start.2
  318.9 1.7 copy-start.7
  321.9 43.7 %copy-start.3 = (f32[320,640]{1,0:T(8,128)S(1)}, f32[320,640]{1,0:T(8,128)}, u32[]{:S(2)}) copy-start(f32[320,640]{1,0:T(8,128)} %param.17) | copy-start | bytes 2457604
  359.8 47.7 %all-to-all-start.1 = ((bf16[128,16,320]{0,2,1:T(8,128)(2,1)}), bf16[128,16,320]{0,2,1:T(8,128)(2,1)}, u32[]{:S(2)}, u32[]{:S(2)}) async-start(bf16[128,16,320]{0,2,1:T(8,128)(2,1)} %bitcast.27), calls=%async_computation.1 | async-start | bytes 2621440 | tf_op jit(solution)/shard_map/all_to_all | solution.py:163
  367.0 2.5 copy-start.4
  482.1 25.6 %all-to-all-start.5 = ((bf16[8,128,640]{2,1,0:T(8,128)(2,1)}), bf16[8,128,640]{2,1,0:T(8,128)(2,1)}, u32[]{:S(2)}, u32[]{:S(2)}) async-start(bf16[8,128,640]{2,1,0:T(8,128)(2,1)} %broadcast_in_dim.71), calls=%async_computation.5 | async-start | bytes 2621440 | tf_op jit(solution)/shard_map/all_to_all | solution.py:17
Sparse Core Ops, SparseCore 0:
  298.0 105.2 reduce-scatter.3
